TPU v7x, 32 devices: a whole 2x2x4 slice. The times are simulated.
32 devices in a mesh: dom: 8 (over z, x), dir: 4 (over y, core).
Axes of the slice: x: 2, y: 2, z: 4, core: 2. Of those that a mesh axis runs over, the one named last changes fastest.
Arguments:
- x_edges: bfloat16 [65536, 128], P(('dom', 'dir')), may hold values from -6 to 6
- send_list: int32 [1024, 32], P(('dom', 'dir')), may hold values from 0 to 2048, as said below
- connectivity: int32 [6, 32768], P(None, ('dom', 'dir')), may hold values from 0 to 3071, as said below
- elem_mats: float32 [36, 32768], P(None, ('dom', 'dir'))
- elem_live: int32 [32], P(('dom', 'dir')), may hold values from 512 to 1024, as said below
- currents: bfloat16 [1024, 128, 128], P(('dom', 'dir')), may hold values from -0.1796875 to 0.1796875
- positions: bfloat16 [1024, 3, 128], P(('dom', 'dir')), may hold values from -1 to 1
- block_live: int32 [1024], P(('dom', 'dir')), may hold values from 32 to 128
- block_owner: int32 [1024], P(('dom', 'dir')), may hold values from 0 to 7, as said below
- block_leaf: int32 [1024], P(('dom', 'dir')), may hold values from 0 to 15
- cone_waves: float32 [3, 16], P(None, 'dir'), may hold values from -6 to 6
Outputs:
- interior_out: float32 [65536, 128], P(('dom', 'dir'))
- expansions: float32 [16, 16, 2, 64, 128], P('dom', 'dir')
Inputs may be any that keep to these rules, and one draw needn't show every extreme that they name: `send_list`: in row a * 32 + b the used entries come first and name owned edges of a; the rest are 2048. A partition reads nothing of itself; some pair uses all 32 entries. `connectivity`: entries below 2048 are owned edges; 2048 + p * 32 + s names the s-th edge that partition p lists for this partition, and only used entries are named. `elem_live`: elements at positions from this count on are padding; some partition has all 1024. `block_owner`: among the 32 blocks of one partition at most 12 name one leaf owner; some leaf owner is named by exactly 12 blocks of every partition.
All inputs are finite; a program needn't handle non-finite values.
Results may differ from a plain program's by a relative error of at most 0.0056.
Values may be sent and summed in bfloat16 or wider, within the bound.
A program may use at most 128 MiB of HBM per device.

v0:
```python
import jax
import jax.numpy as jnp
from jax import lax
from jax.sharding import PartitionSpec as P

LEAVES_DEV = 16
NODES = 4


def cheb_points():
    node_order = jnp.arange(NODES).astype(jnp.float32)
    return jnp.cos((2.0 * node_order + 1.0) * (jnp.pi / (2.0 * NODES)))


def lagrange(points):
    node_values = cheb_points()
    rows_out = []
    for target in range(NODES):
        product = jnp.ones_like(points)
        for other_node in range(NODES):
            if other_node != target:
                product = (
                    product
                    * (points - node_values[other_node])
                    / (node_values[target] - node_values[other_node])
                )
        rows_out.append(product)
    return jnp.stack(rows_out, axis=-2)


def tensor_basis(coords):
    first = lagrange(coords[..., 0, :])
    second = lagrange(coords[..., 1, :])
    third = lagrange(coords[..., 2, :])
    joined = (
        first[..., :, None, None, :] * second[..., None, :, None, :] * third[..., None, None, :, :]
    )
    return joined.reshape(coords.shape[:-2] + (NODES**3, coords.shape[-1]))


def node_coords():
    ladder = jnp.arange(NODES**3)
    digits = jnp.stack([ladder // (NODES * NODES), ladder // NODES % NODES, ladder % NODES]).astype(
        jnp.float32
    )
    return jnp.cos((2.0 * digits + 1.0) * (jnp.pi / (2.0 * NODES)))


def wave_phase(waves, coords):
    return (
        waves[0][:, None] * coords[..., None, 0, :]
        + waves[1][:, None] * coords[..., None, 1, :]
        + waves[2][:, None] * coords[..., None, 2, :]
    )


def m2m_tables(waves):
    octant = jnp.arange(8)
    shifts = jnp.stack([octant // 4, octant // 2 % 2, octant % 2], axis=1).astype(jnp.float32) - 0.5
    points = shifts[:, :, None] + 0.5 * cheb_points()[None, None, :]
    weights = lagrange(points)
    first = weights[:, 0]
    second = weights[:, 1]
    third = weights[:, 2]
    joined = (
        first[:, :, None, None, :, None, None]
        * second[:, None, :, None, None, :, None]
        * third[:, None, None, :, None, None, :]
    )
    square = NODES**3
    joined = joined.reshape(8, square, square)
    child = shifts[:, :, None] + 0.5 * node_coords()[None]
    spread = child[:, :, None, :] - node_coords()[None, :, :, None]
    psi = 2.0 * (
        waves[0][:, None, None, None] * spread[None, :, 0]
        + waves[1][:, None, None, None] * spread[None, :, 1]
        + waves[2][:, None, None, None] * spread[None, :, 2]
    )
    table_real = (joined[None] * jnp.cos(psi)).astype(jnp.bfloat16)
    table_imag = (-joined[None] * jnp.sin(psi)).astype(jnp.bfloat16)
    return (table_real, table_imag)


def pack_slots(owners, dest_count, capacity, members):
    matches = (owners[:, None] == jnp.arange(dest_count)[None, :]).astype(jnp.int32)
    ranking = jnp.sum((jnp.cumsum(matches, axis=0) - matches) * matches, axis=1)
    slot_index = owners * capacity + ranking
    source_row = (
        jnp.full((dest_count * capacity,), owners.shape[0], jnp.int32)
        .at[slot_index]
        .set(jnp.arange(owners.shape[0], dtype=jnp.int32))
    )
    padded = [
        jnp.concatenate([member, jnp.zeros((1,) + member.shape[1:], member.dtype)])
        for member in members
    ]
    return tuple((array_now[source_row] for array_now in padded))


def interior_part(x_edges, send_list, connectivity, elem_mats, elem_live):
    owned_rows, columns = x_edges.shape
    partitions, slot_width = send_list.shape
    element_count = connectivity.shape[1]
    padded = jnp.concatenate([x_edges, jnp.zeros((1, columns), x_edges.dtype)])
    outgoing = padded[send_list]
    received = lax.all_to_all(outgoing, ("dom", "dir"), split_axis=0, concat_axis=0, tiled=True)
    edge_table = jnp.concatenate([x_edges, received.reshape(partitions * slot_width, columns)])
    gathered = edge_table[connectivity]
    live_mask = (jnp.arange(element_count) < elem_live[0])[:, None]
    term_list = []
    for row_index in range(6):
        summed = jnp.zeros((element_count, columns), jnp.float32)
        for col_index in range(6):
            summed = summed + elem_mats[row_index * 6 + col_index][:, None] * gathered[col_index]
        term_list.append(jnp.where(live_mask, summed, jnp.zeros_like(summed)))
    stacked = jnp.stack(term_list).reshape(6 * element_count, columns)
    assembled = jax.ops.segment_sum(
        stacked, connectivity.reshape(-1), num_segments=owned_rows + partitions * slot_width
    )
    back_terms = assembled[owned_rows:]
    returned = lax.all_to_all(
        back_terms.reshape(partitions, slot_width, columns),
        ("dom", "dir"),
        split_axis=0,
        concat_axis=0,
        tiled=True,
    )
    folded = jax.ops.segment_sum(
        returned.reshape(-1, columns), send_list.reshape(-1), num_segments=owned_rows + 1
    )
    return assembled[:owned_rows] + folded[:owned_rows]


def expand_leaves(arrived_blocks, arrived_meta, waves):
    block_size = arrived_blocks.shape[1]
    columns = arrived_blocks.shape[2]
    cone_count = waves.shape[1]
    square = NODES**3
    group_rows = 512 // cone_count
    group_count = arrived_blocks.shape[0] // group_rows
    leaf_ids = arrived_meta[:, 3, 0].astype(jnp.int32)

    def one_group(carry, inputs):
        real_sum, imag_sum = carry
        blocks_now, coords, leaves = inputs
        coords_wide = coords.astype(jnp.float32)
        basis_now = tensor_basis(coords_wide)
        phase_now = wave_phase(waves, coords_wide)
        real_w = (basis_now[:, None] * jnp.cos(phase_now)[:, :, None, :]).astype(jnp.bfloat16)
        imag_w = (-basis_now[:, None] * jnp.sin(phase_now)[:, :, None, :]).astype(jnp.bfloat16)
        real_part = jnp.einsum(
            "gcqb,gbn->gcqn", real_w, blocks_now, preferred_element_type=jnp.float32
        ).astype(jnp.bfloat16)
        imag_part = jnp.einsum(
            "gcqb,gbn->gcqn", imag_w, blocks_now, preferred_element_type=jnp.float32
        ).astype(jnp.bfloat16)
        selector = (jnp.arange(LEAVES_DEV)[:, None] == leaves[None, :]).astype(jnp.bfloat16)
        real_sum = real_sum + jnp.einsum(
            "lg,gcqn->lcqn", selector, real_part, preferred_element_type=jnp.float32
        )
        imag_sum = imag_sum + jnp.einsum(
            "lg,gcqn->lcqn", selector, imag_part, preferred_element_type=jnp.float32
        )
        return ((real_sum, imag_sum), None)

    empty = jnp.zeros((LEAVES_DEV, cone_count, square, columns), jnp.float32)
    inputs = (
        arrived_blocks.reshape(group_count, group_rows, block_size, columns),
        arrived_meta[:, :3].reshape(group_count, group_rows, 3, block_size),
        leaf_ids.reshape(group_count, group_rows),
    )
    sums, unused = lax.scan(one_group, (empty, empty), inputs)
    real_sum, imag_sum = sums
    node_phase = wave_phase(waves, node_coords())
    cosine = jnp.cos(node_phase)[None, :, :, None]
    sine_part = jnp.sin(node_phase)[None, :, :, None]
    leaf_real = (cosine * real_sum - sine_part * imag_sum).astype(jnp.bfloat16)
    leaf_imag = (cosine * imag_sum + sine_part * real_sum).astype(jnp.bfloat16)
    table_real, table_imag = m2m_tables(waves)
    child_real = leaf_real.reshape(LEAVES_DEV // 8, 8, cone_count, square, columns)
    child_imag = leaf_imag.reshape(LEAVES_DEV // 8, 8, cone_count, square, columns)
    parent_real = jnp.einsum(
        "cops,xocsn->xcpn", table_real, child_real, preferred_element_type=jnp.float32
    ) - jnp.einsum("cops,xocsn->xcpn", table_imag, child_imag, preferred_element_type=jnp.float32)
    parent_imag = jnp.einsum(
        "cops,xocsn->xcpn", table_real, child_imag, preferred_element_type=jnp.float32
    ) + jnp.einsum("cops,xocsn->xcpn", table_imag, child_real, preferred_element_type=jnp.float32)
    return jnp.stack([parent_real, parent_imag], axis=2)


def boundary_part(currents, positions, block_live, block_owner, block_leaf, cone_waves):
    block_count, block_size, columns = currents.shape
    dom_count = lax.axis_size("dom")
    capacity = 3 * block_count // dom_count
    live_mask = jnp.arange(block_size)[None, :] < block_live[:, None]
    masked = jnp.where(live_mask[:, :, None], currents, jnp.zeros_like(currents))
    leaf_row = jnp.broadcast_to(
        block_leaf.astype(jnp.bfloat16)[:, None, None], (block_count, 1, block_size)
    )
    described = jnp.concatenate([positions, leaf_row], axis=1)
    packed_blocks, packed_meta = pack_slots(block_owner, dom_count, capacity, (masked, described))
    owner_blocks, owner_meta = (
        lax.all_to_all(packed_blocks, "dom", split_axis=0, concat_axis=0, tiled=True),
        lax.all_to_all(packed_meta, "dom", split_axis=0, concat_axis=0, tiled=True),
    )
    arrived_blocks, arrived_meta = (
        lax.all_gather(owner_blocks, "dir", axis=0, tiled=True),
        lax.all_gather(owner_meta, "dir", axis=0, tiled=True),
    )
    parents = expand_leaves(arrived_blocks, arrived_meta, cone_waves)
    return parents


def shards(
    x_edges,
    send_list,
    connectivity,
    elem_mats,
    elem_live,
    currents,
    positions,
    block_live,
    block_owner,
    block_leaf,
    cone_waves,
):
    interior_out = interior_part(x_edges, send_list, connectivity, elem_mats, elem_live)
    expansions = boundary_part(currents, positions, block_live, block_owner, block_leaf, cone_waves)
    return (interior_out, expansions)


def solution(mesh):
    placed = (
        P(("dom", "dir"), None),
        P(("dom", "dir"), None),
        P(None, ("dom", "dir")),
        P(None, ("dom", "dir")),
        P(("dom", "dir")),
        P(("dom", "dir"), None, None),
        P(("dom", "dir"), None, None),
        P(("dom", "dir")),
        P(("dom", "dir")),
        P(("dom", "dir")),
        P(None, "dir"),
    )
    return jax.shard_map(
        shards,
        mesh=mesh,
        in_specs=placed,
        out_specs=(P(("dom", "dir"), None), P("dom", "dir", None, None, None)),
        check_vma=False,
    )
```

profile of v0, /device:TPU:1, one launch (start us, length us, event | category | flops | bytes accessed | tf_op | source)
XLA Modules:
  0.0 447.2 jit_solution(9750463956113787339)
XLA Ops:
  13.6 2.7 gather_fusion.3
  16.3 76.3 %all_to_all.20 = bf16[96,128,128]{2,1,0:T(8,128)(2,1)} all-to-all(bf16[96,128,128]{2,1,0:T(8,128)(2,1)} %gather_fusion.3), channel_id=1, replica_groups=mesh['dom'=8,'dir'=4] {'dom'}, dimensions={0} | all-to-all | bytes 6291456 | tf_op jit(solution)/shard_map/all_to_all | solution.py:203
  93.6 4.3 gather_fusion
  97.9 5.2 %all-to-all-start = ((bf16[32,32,128]{2,1,0:T(8,128)(2,1)}), bf16[32,32,128]{2,1,0:T(8,128)(2,1)S(1)}, u32[]{:S(2)}, u32[]{:S(2)}) async-start(bf16[32,32,128]{2,1,0:T(8,128)(2,1)} %bitcast.2), calls=%async_computation | async-start | bytes 524288 | tf_op jit(solution)/shard_map/all_to_all | solution.py:106
  119.4 2.5 fusion.102
  127.2 1.8 copy.37
  130.4 3.3 copy.39
  134.5 5.7 %all-to-all-start.2 = ((bf16[96,4,128]{2,1,0:T(4,128)(2,1)}), bf16[96,4,128]{2,1,0:T(4,128)(2,1)S(1)}, u32[]{:S(2)}, u32[]{:S(2)}) async-start(bf16[96,4,128]{2,1,0:T(4,128)(2,1)} %gather_fusion.2), calls=%async_computation.2 | async-start | bytes 196608 | tf_op jit(solution)/shard_map/all_to_all | solution.py:204
  140.3 18.1 %gather_fusion.1 = bf16[6144,128]{1,0:T(8,128)(2,1)S(1)} fusion(bf16[3072,128]{1,0:T(8,128)(2,1)S(1)} %pad_maximum_fusion.3, s32[6144]{0:T(1024)S(1)} %broadcast_clamp_fusion), kind=kCustom, calls=%fused_computation.1 | custom fusion | bytes 3170304 | tf_op jit(solution)/shard_map/gather | solution.py:108
  168.0 33.9 %scatter_custom_fusion = f32[3072,128]{1,0:T(8,128)S(1)} fusion(s32[6144]{0:T(1024)} %reshape.1056, f32[6144,128]{1,0:T(8,128)} %bitcast.296, f32[]{:T(128)} %constant.151.clone.1), kind=kCustom, calls=%fused_computation.118 | custom fusion | flops 786432 | bytes 1573376 | tf_op jit(solution)/shard_map/scatter-add | solution.py:117
  202.8 6.4 %all-to-all-start.1 = ((f32[32,32,128]{2,1,0:T(8,128)}), f32[32,32,128]{2,1,0:T(8,128)S(1)}, u32[]{:S(2)}, u32[]{:S(2)}) async-start(f32[32,32,128]{2,1,0:T(8,128)} %bitcast.52), calls=%async_computation.1 | async-start | bytes 1048576 | tf_op jit(solution)/shard_map/all_to_all | solution.py:121
  210.6 9.4 %all_gather.6 = bf16[384,4,128]{2,1,0:T(4,128)(2,1)S(1)} all-gather(bf16[96,4,128]{2,1,0:T(4,128)(2,1)S(1)} %all-to-all-done.2), channel_id=1, replica_groups=mesh['dom'=8,'dir'=4] {'dir'}, dimensions={0}, use_global_device_ids=true | all-gather | bytes 491520 | tf_op jit(solution)/shard_map/all_gather | solution.py:208
  220.1 6.9 %fusion.84 = s32[384]{0:T(512)S(1)} fusion(bf16[384,4,128]{2,1,0:T(4,128)(2,1)S(1)} %all_gather.6), kind=kLoop, calls=%fused_computation.178 | loop fusion | flops 384 | bytes 2304 | tf_op jit(solution)/shard_map/convert_element_type | solution.py:141
  227.8 7.3 %scatter_custom_fusion.1 = f32[2049,128]{1,0:T(8,128)S(1)} fusion(s32[1024]{0:T(1024)} %reshape.1064, f32[1024,128]{1,0:T(8,128)} %bitcast.295, f32[]{:T(128)} %constant.151.clone.1), kind=kCustom, calls=%fused_computation.120 | custom fusion | flops 131072 | bytes 1049600 | tf_op jit(solution)/shard_map/scatter-add | solution.py:128
  235.0 2.3 slice_add_fusion
  237.3 183.9 %while.13 = (s32[]{:T(128)}, f32[16,4,64,128]{3,0,2,1:T(8,128)S(1)}, f32[16,4,64,128]{3,0,2,1:T(8,128)}, s32[3,128]{1,0:T(4,128)S(1)}, bf16[3,128,3,128]{3,1,2,0...) while((s32[]{:T(128)}, ...), condition=%wide.region_6.7_spmd.clone, body=%wide.region_5.6_spmd.clone.sunk | while | flops 2447904768 | bytes 113871504 | solution.py:172
  260.6 2.6 multiply_divide_fusion.15
  267.0 2.6 multiply_divide_fusion.16
  269.6 2.1 fusion.150
  271.7 2.6 multiply_divide_fusion.17
  276.5 2.0 copy-done
  278.5 6.9 %fusion.151 = bf16[128,4,64,128]{3,2,1,0:T(8,128)(2,1)} fusion(f32[128,4,128]{2,1,0:T(4,128)S(1)} %get-tuple-element.266, f32[128,64,128]{2,1,0:T(8,128)S(1)} %bitcast.288, bf16[3,128,128,128]{3,2,1,0:T(8,128)(2,1)} %get-tuple-element.306, s32[]{:T(128)S(6)} %copy.78), kind=kOutput, calls=%fused_computation.20.clone.1 | convolution fusion | flops 1086324736 | bytes 17039364 | tf_op jit(solution)/shard_map/while/body/eval_jaxpr/gcqb,gbn->gcqn/dot_general | solution.py:151
  285.5 8.2 %select_add_fusion.4 = f32[16,4,64,128]{3,0,2,1:T(8,128)S(1)} fusion(f32[16,4,64,128]{3,0,2,1:T(8,128)S(1)} %get-tuple-element.292, bf16[128,4,64,128]{3,2,1,0:T(8,128)(2,1)} %fusion.151, pred[]{:T(512)S(6)} %compare.55, s32[128]{0:T(128)S(1)} %fusion.152), kind=kOutput, calls=%fused_computation.26.clone.1 | convolution fusion | flops 135268352 | bytes 12583425 | tf_op jit(solution)/shard_map/while/body/eval_jaxpr/lg,gcqn->lcqn/dot_general | solution.py:158
  294.1 4.8 %fusion.153 = bf16[128,4,64,128]{3,2,1,0:T(8,128)(2,1)S(1)} fusion(f32[128,4,128]{2,1,0:T(4,128)S(1)} %get-tuple-element.281, f32[128,64,128]{2,1,0:T(8,128)S(1)} %neg.19, bf16[3,128,128,128]{3,2,1,0:T(8,128)(2,1)} %get-tuple-element.306, s32[]{:T(128)S(6)} %copy.78), kind=kOutput, calls=%fused_computation.19.clone.1 | convolution fusion | flops 1086324736 | bytes 17039364 | tf_op jit(solution)/shard_map/while/body/eval_jaxpr/gcqb,gbn->gcqn/dot_general | solution.py:154
  299.0 6.0 %select_add_fusion.5 = f32[16,4,64,128]{3,0,2,1:T(8,128)} fusion(f32[16,4,64,128]{3,0,2,1:T(8,128)} %get-tuple-element.293, bf16[128,4,64,128]{3,2,1,0:T(8,128)(2,1)S(1)} %fusion.153, pred[]{:T(512)S(6)} %compare.55, s32[128]{0:T(128)S(1)} %fusion.152), kind=kOutput, calls=%fused_computation.25.clone.1 | convolution fusion | flops 135268352 | bytes 12583425 | tf_op jit(solution)/shard_map/while/body/eval_jaxpr/lg,gcqn->lcqn/dot_general | solution.py:161
  317.0 2.6 multiply_divide_fusion.15
  323.4 2.6 multiply_divide_fusion.16
  326.0 2.1 fusion.150
  328.1 2.6 multiply_divide_fusion.17
  332.9 2.0 copy-done
  335.0 6.9 %fusion.151 = bf16[128,4,64,128]{3,2,1,0:T(8,128)(2,1)} fusion(f32[128,4,128]{2,1,0:T(4,128)S(1)} %get-tuple-element.266, f32[128,64,128]{2,1,0:T(8,128)S(1)} %bitcast.288, bf16[3,128,128,128]{3,2,1,0:T(8,128)(2,1)} %get-tuple-element.306, s32[]{:T(128)S(6)} %copy.78), kind=kOutput, calls=%fused_computation.20.clone.1 | convolution fusion | flops 1086324736 | bytes 17039364 | tf_op jit(solution)/shard_map/while/body/eval_jaxpr/gcqb,gbn->gcqn/dot_general | solution.py:151
  341.9 8.2 %select_add_fusion.4 = f32[16,4,64,128]{3,0,2,1:T(8,128)S(1)} fusion(f32[16,4,64,128]{3,0,2,1:T(8,128)S(1)} %get-tuple-element.292, bf16[128,4,64,128]{3,2,1,0:T(8,128)(2,1)} %fusion.151, pred[]{:T(512)S(6)} %compare.55, s32[128]{0:T(128)S(1)} %fusion.152), kind=kOutput, calls=%fused_computation.26.clone.1 | convolution fusion | flops 135268352 | bytes 12583425 | tf_op jit(solution)/shard_map/while/body/eval_jaxpr/lg,gcqn->lcqn/dot_general | solution.py:158
  350.6 4.8 %fusion.153 = bf16[128,4,64,128]{3,2,1,0:T(8,128)(2,1)S(1)} fusion(f32[128,4,128]{2,1,0:T(4,128)S(1)} %get-tuple-element.281, f32[128,64,128]{2,1,0:T(8,128)S(1)} %neg.19, bf16[3,128,128,128]{3,2,1,0:T(8,128)(2,1)} %get-tuple-element.306, s32[]{:T(128)S(6)} %copy.78), kind=kOutput, calls=%fused_computation.19.clone.1 | convolution fusion | flops 1086324736 | bytes 17039364 | tf_op jit(solution)/shard_map/while/body/eval_jaxpr/gcqb,gbn->gcqn/dot_general | solution.py:154
  355.4 7.6 %select_add_fusion.5 = f32[16,4,64,128]{3,0,2,1:T(8,128)} fusion(f32[16,4,64,128]{3,0,2,1:T(8,128)} %get-tuple-element.293, bf16[128,4,64,128]{3,2,1,0:T(8,128)(2,1)S(1)} %fusion.153, pred[]{:T(512)S(6)} %compare.55, s32[128]{0:T(128)S(1)} %fusion.152), kind=kOutput, calls=%fused_computation.25.clone.1 | convolution fusion | flops 135268352 | bytes 12583425 | tf_op jit(solution)/shard_map/while/body/eval_jaxpr/lg,gcqn->lcqn/dot_general | solution.py:161
  375.1 2.6 multiply_divide_fusion.15
  381.5 2.6 multiply_divide_fusion.16
  384.1 2.1 fusion.150
  386.1 2.6 multiply_divide_fusion.17
  391.0 2.0 copy-done
  393.0 6.9 %fusion.151 = bf16[128,4,64,128]{3,2,1,0:T(8,128)(2,1)} fusion(f32[128,4,128]{2,1,0:T(4,128)S(1)} %get-tuple-element.266, f32[128,64,128]{2,1,0:T(8,128)S(1)} %bitcast.288, bf16[3,128,128,128]{3,2,1,0:T(8,128)(2,1)} %get-tuple-element.306, s32[]{:T(128)S(6)} %copy.78), kind=kOutput, calls=%fused_computation.20.clone.1 | convolution fusion | flops 1086324736 | bytes 17039364 | tf_op jit(solution)/shard_map/while/body/eval_jaxpr/gcqb,gbn->gcqn/dot_general | solution.py:151
  399.9 8.2 %select_add_fusion.4 = f32[16,4,64,128]{3,0,2,1:T(8,128)S(1)} fusion(f32[16,4,64,128]{3,0,2,1:T(8,128)S(1)} %get-tuple-element.292, bf16[128,4,64,128]{3,2,1,0:T(8,128)(2,1)} %fusion.151, pred[]{:T(512)S(6)} %compare.55, s32[128]{0:T(128)S(1)} %fusion.152), kind=kOutput, calls=%fused_computation.26.clone.1 | convolution fusion | flops 135268352 | bytes 12583425 | tf_op jit(solution)/shard_map/while/body/eval_jaxpr/lg,gcqn->lcqn/dot_general | solution.py:158
  408.6 4.8 %fusion.153 = bf16[128,4,64,128]{3,2,1,0:T(8,128)(2,1)S(1)} fusion(f32[128,4,128]{2,1,0:T(4,128)S(1)} %get-tuple-element.281, f32[128,64,128]{2,1,0:T(8,128)S(1)} %neg.19, bf16[3,128,128,128]{3,2,1,0:T(8,128)(2,1)} %get-tuple-element.306, s32[]{:T(128)S(6)} %copy.78), kind=kOutput, calls=%fused_computation.19.clone.1 | convolution fusion | flops 1086324736 | bytes 17039364 | tf_op jit(solution)/shard_map/while/body/eval_jaxpr/gcqb,gbn->gcqn/dot_general | solution.py:154
  413.4 7.6 %select_add_fusion.5 = f32[16,4,64,128]{3,0,2,1:T(8,128)} fusion(f32[16,4,64,128]{3,0,2,1:T(8,128)} %get-tuple-element.293, bf16[128,4,64,128]{3,2,1,0:T(8,128)(2,1)S(1)} %fusion.153, pred[]{:T(512)S(6)} %compare.55, s32[128]{0:T(128)S(1)} %fusion.152), kind=kOutput, calls=%fused_computation.25.clone.1 | convolution fusion | flops 135268352 | bytes 12583425 | tf_op jit(solution)/shard_map/while/body/eval_jaxpr/lg,gcqn->lcqn/dot_general | solution.py:161
  421.3 2.1 fusion.35
  423.5 3.8 convolution_bitcast_fusion
  427.3 3.8 convolution_bitcast_fusion.2
  431.1 3.8 fusion.33
  435.0 4.1 fusion.31
  (226 shorter events, 39.1 us)
Async XLA Ops:
  7.2 230.2 %all-gather.2.cloned.1.call-start = ((), (), s32[]{:S(2)}) async-start(), calls=%async_computation.4 | async-start | bytes 15728640 | tf_op jit(solution)/shard_map/all_gather | solution.py:207
  92.5 26.6 %copy-start.12 = (s32[6,1024]{1,0:T(8,128)S(1)}, s32[6,1024]{1,0:T(8,128)}, u32[]{:S(2)}) copy-start(s32[6,1024]{1,0:T(8,128)} %param.15) | copy-start | bytes 73732
  92.5 26.6 %copy-start.57 = (s32[32]{0:T(128)S(1)}, s32[32]{0:T(128)}, u32[]{:S(2)}) copy-start(s32[32]{0:T(128)} %param.22) | copy-start | bytes 388
  92.5 26.6 %copy-start.16 = (bf16[32,3,128]{2,0,1:T(8,128)(2,1)S(1)}, bf16[32,3,128]{2,0,1:T(8,128)(2,1)}, u32[]{:S(2)}) copy-start(bf16[32,3,128]{2,0,1:T(8,128)(2,1)} %param.19) | copy-start | bytes 73732
  92.5 30.1 %copy-start.15 = (f32[3,4]{1,0:T(4,128)S(1)}, f32[3,4]{1,0:T(4,128)}, u32[]{:S(2)}) copy-start(f32[3,4]{1,0:T(4,128)} %param.23) | copy-start | bytes 148
  92.5 30.7 %copy-start.11 = (f32[36,1024]{1,0:T(8,128)S(1)}, f32[36,1024]{1,0:T(8,128)}, u32[]{:S(2)}) copy-start(f32[36,1024]{1,0:T(8,128)} %param.16) | copy-start | bytes 442372
  93.6 30.9 %copy-start.14 = (s32[32,32]{1,0:T(8,128)S(1)}, s32[32,32]{1,0:T(8,128)}, u32[]{:S(2)}) copy-start(s32[32,32]{1,0:T(8,128)} %param.14) | copy-start | bytes 12292
  97.9 36.6 %all-to-all-start = ((bf16[32,32,128]{2,1,0:T(8,128)(2,1)}), bf16[32,32,128]{2,1,0:T(8,128)(2,1)S(1)}, u32[]{:S(2)}, u32[]{:S(2)}) async-start(bf16[32,32,128]{2,1,0:T(8,128)(2,1)} %bitcast.2), calls=%async_computation | async-start | bytes 524288 | tf_op jit(solution)/shard_map/all_to_all | solution.py:106
  119.3 7.9 %copy-start.49 = (f32[3,64]{1,0:T(4,128)}, f32[3,64]{1,0:T(4,128)S(1)}, u32[]{:S(2)}) copy-start(f32[3,64]{1,0:T(4,128)S(1)} %get-tuple-element.176) | copy-start | bytes 2308
  134.5 68.3 %all-to-all-start.2 = ((bf16[96,4,128]{2,1,0:T(4,128)(2,1)}), bf16[96,4,128]{2,1,0:T(4,128)(2,1)S(1)}, u32[]{:S(2)}, u32[]{:S(2)}) async-start(bf16[96,4,128]{2,1,0:T(4,128)(2,1)} %gather_fusion.2), calls=%async_computation.2 | async-start | bytes 196608 | tf_op jit(solution)/shard_map/all_to_all | solution.py:204
  140.2 18.3 %copy-start.24 = (f32[1,1024]{1,0:T(1,128)S(1)}, f32[1,1024]{1,0:T(1,128)}, u32[]{:S(2)}) copy-start(f32[1,1024]{1,0:T(1,128)} %get-tuple-element.153) | copy-start | bytes 12292
  140.2 18.3 %copy-start.25 = (f32[1,1024]{1,0:T(1,128)S(1)}, f32[1,1024]{1,0:T(1,128)}, u32[]{:S(2)}) copy-start(f32[1,1024]{1,0:T(1,128)} %get-tuple-element.154) | copy-start | bytes 12292
  140.2 18.3 %copy-start.26 = (f32[1,1024]{1,0:T(1,128)S(1)}, f32[1,1024]{1,0:T(1,128)}, u32[]{:S(2)}) copy-start(f32[1,1024]{1,0:T(1,128)} %get-tuple-element.155) | copy-start | bytes 12292
  140.2 18.3 %copy-start.27 = (f32[1,1024]{1,0:T(1,128)S(1)}, f32[1,1024]{1,0:T(1,128)}, u32[]{:S(2)}) copy-start(f32[1,1024]{1,0:T(1,128)} %get-tuple-element.156) | copy-start | bytes 12292
  140.3 18.3 %copy-start.28 = (f32[1,1024]{1,0:T(1,128)S(1)}, f32[1,1024]{1,0:T(1,128)}, u32[]{:S(2)}) copy-start(f32[1,1024]{1,0:T(1,128)} %get-tuple-element.157) | copy-start | bytes 12292
  140.3 18.3 %copy-start.29 = (f32[1,1024]{1,0:T(1,128)S(1)}, f32[1,1024]{1,0:T(1,128)}, u32[]{:S(2)}) copy-start(f32[1,1024]{1,0:T(1,128)} %get-tuple-element.158) | copy-start | bytes 12292
  140.3 19.5 %copy-start.18 = (f32[1,1024]{1,0:T(1,128)S(1)}, f32[1,1024]{1,0:T(1,128)}, u32[]{:S(2)}) copy-start(f32[1,1024]{1,0:T(1,128)} %get-tuple-element.147) | copy-start | bytes 12292
  140.3 19.5 %copy-start.19 = (f32[1,1024]{1,0:T(1,128)S(1)}, f32[1,1024]{1,0:T(1,128)}, u32[]{:S(2)}) copy-start(f32[1,1024]{1,0:T(1,128)} %get-tuple-element.148) | copy-start | bytes 12292
  140.3 19.5 %copy-start.20 = (f32[1,1024]{1,0:T(1,128)S(1)}, f32[1,1024]{1,0:T(1,128)}, u32[]{:S(2)}) copy-start(f32[1,1024]{1,0:T(1,128)} %get-tuple-element.149) | copy-start | bytes 12292
  140.3 19.5 %copy-start.21 = (f32[1,1024]{1,0:T(1,128)S(1)}, f32[1,1024]{1,0:T(1,128)}, u32[]{:S(2)}) copy-start(f32[1,1024]{1,0:T(1,128)} %get-tuple-element.150) | copy-start | bytes 12292
  140.3 19.5 %copy-start.22 = (f32[1,1024]{1,0:T(1,128)S(1)}, f32[1,1024]{1,0:T(1,128)}, u32[]{:S(2)}) copy-start(f32[1,1024]{1,0:T(1,128)} %get-tuple-element.151) | copy-start | bytes 12292
  140.3 19.5 %copy-start.23 = (f32[1,1024]{1,0:T(1,128)S(1)}, f32[1,1024]{1,0:T(1,128)}, u32[]{:S(2)}) copy-start(f32[1,1024]{1,0:T(1,128)} %get-tuple-element.152) | copy-start | bytes 12292
  158.5 3.9 copy-start.40
  158.5 3.9 copy-start.41
  158.5 3.9 copy-start.42
  158.6 3.9 copy-start.43
  158.6 3.9 copy-start.44
  158.6 3.9 copy-start.45
  159.9 3.9 copy-start.34
  159.9 3.9 copy-start.35
  161.2 3.9 copy-start.30
  161.2 3.9 copy-start.31
  161.2 3.9 copy-start.32
  161.2 3.9 copy-start.33
  165.0 44.2 %copy-start.51 = (f32[4]{0:T(128)S(1)}, f32[4]{0:T(128)}, u32[]{:S(2)}) copy-start(f32[4]{0:T(128)} %get-tuple-element.169) | copy-start | bytes 52
  165.0 44.2 %copy-start.52 = (f32[4]{0:T(128)S(1)}, f32[4]{0:T(128)}, u32[]{:S(2)}) copy-start(f32[4]{0:T(128)} %get-tuple-element.170) | copy-start | bytes 52
  165.0 44.2 %copy-start.53 = (f32[4]{0:T(128)S(1)}, f32[4]{0:T(128)}, u32[]{:S(2)}) copy-start(f32[4]{0:T(128)} %get-tuple-element.171) | copy-start | bytes 52
  165.0 44.2 %copy-start.54 = (f32[64]{0:T(128)S(1)}, f32[64]{0:T(128)}, u32[]{:S(2)}) copy-start(f32[64]{0:T(128)} %get-tuple-element.172) | copy-start | bytes 772
  165.1 44.2 %copy-start.55 = (f32[64]{0:T(128)S(1)}, f32[64]{0:T(128)}, u32[]{:S(2)}) copy-start(f32[64]{0:T(128)} %get-tuple-element.173) | copy-start | bytes 772
  165.1 44.2 %copy-start.56 = (f32[64]{0:T(128)S(1)}, f32[64]{0:T(128)}, u32[]{:S(2)}) copy-start(f32[64]{0:T(128)} %get-tuple-element.174) | copy-start | bytes 772
  165.1 44.3 %copy-start.50 = (f32[3,64]{1,0:T(4,128)S(1)}, f32[3,64]{1,0:T(4,128)}, u32[]{:S(2)}) copy-start(f32[3,64]{1,0:T(4,128)} %copy-done.49) | copy-start | bytes 2308
  201.9 7.8 %copy-start.3 = (f32[3072,128]{1,0:T(8,128)}, f32[3072,128]{1,0:T(8,128)S(1)}, u32[]{:S(2)}) copy-start(f32[3072,128]{1,0:T(8,128)S(1)} %scatter_custom_fusion) | copy-start | bytes 4718596
  202.8 24.1 %all-to-all-start.1 = ((f32[32,32,128]{2,1,0:T(8,128)}), f32[32,32,128]{2,1,0:T(8,128)S(1)}, u32[]{:S(2)}, u32[]{:S(2)}) async-start(f32[32,32,128]{2,1,0:T(8,128)} %bitcast.52), calls=%async_computation.1 | async-start | bytes 1048576 | tf_op jit(solution)/shard_map/all_to_all | solution.py:121
  210.6 26.7 %copy-start.2 = (f32[16,4,64,128]{3,0,2,1:T(8,128)S(1)}, f32[16,4,64,128]{3,0,2,1:T(8,128)}, u32[]{:S(2)}) copy-start(f32[16,4,64,128]{3,0,2,1:T(8,128)} %custom-call) | copy-start | bytes 6291460
  285.5 8.2 %copy-start.1 = (f32[128,4,4,4,128]{4,3,2,1,0:T(4,128)S(1)}, f32[128,4,4,4,128]{4,3,2,1,0:T(4,128)}, u32[]{:S(2)}) copy-start(f32[128,4,4,4,128]{4,3,2,1,0:T(4,128)} %copy-done) | copy-start | bytes 12582916 | tf_op jit(solution)/shard_map/while
  341.9 8.2 %copy-start.1 = (f32[128,4,4,4,128]{4,3,2,1,0:T(4,128)S(1)}, f32[128,4,4,4,128]{4,3,2,1,0:T(4,128)}, u32[]{:S(2)}) copy-start(f32[128,4,4,4,128]{4,3,2,1,0:T(4,128)} %copy-done) | copy-start | bytes 12582916 | tf_op jit(solution)/shard_map/while
  399.9 8.2 %copy-start.1 = (f32[128,4,4,4,128]{4,3,2,1,0:T(4,128)S(1)}, f32[128,4,4,4,128]{4,3,2,1,0:T(4,128)}, u32[]{:S(2)}) copy-start(f32[128,4,4,4,128]{4,3,2,1,0:T(4,128)} %copy-done) | copy-start | bytes 12582916 | tf_op jit(solution)/shard_map/while
  423.4 7.7 %copy-start.6 = (f32[8,64,64]{1,0,2:T(8,128)S(1)}, f32[8,64,64]{1,0,2:T(8,128)}, u32[]{:S(2)}) copy-start(f32[8,64,64]{1,0,2:T(8,128)} %copy.37) | copy-start | bytes 393220
  (18 other events, 44.6 us)
Sparse Core Ops, SparseCore 0:
  92.7 85.4 all-gather.1
where the time goes:
time: 454 us; the launch traced here: 447 us
  other arithmetic  107 us (24%)
  matrix products  96.7 us (21%)
  blocking collectives  85.7 us (19%)
  loops' own time  57 us (13%)
  local copies, waits for them, and re-layouts  53 us (12%)
  between operations  30.8 us (7%)
  starting transfers between devices  17.3 us (4%)
    all_to_all x1, blocking collectives, boundary_part(): lax.all_to_all(packed_blocks, 'dom', split_axis=0, concat_axis=0, tiled=T...  76.3 us
    another operation x1, loops' own time, expand_leaves(): sums, unused = lax.scan(one_group, (empty, empty), inputs)  57 us
    scatter-add x1, other arithmetic, interior_part(): jax.ops.segment_sum(stacked, connectivity.reshape(-1), num_segments=owned...  33.9 us
    div x10, other arithmetic, lagrange(): product * (points - node_values[other_node])  25.7 us
    dot_general x3, matrix products, one_group(): jnp.einsum('lg,gcqn->lcqn', selector, real_part, preferred_element_type=j...  24.6 us
    dot_general x3, matrix products, one_group(): jnp.einsum('lg,gcqn->lcqn', selector, imag_part, preferred_element_type=j...  21.3 us
    dot_general x3, matrix products, one_group(): jnp.einsum('gcqb,gbn->gcqn', real_w, blocks_now, preferred_element_type=j...  20.8 us
    gather x1, local copies, waits for them, and re-layouts, interior_part(): gathered = edge_table[connectivity]  18.1 us
  transfers between devices with their start and end apart: 4, of which 0 were waited for; matrix products, arithmetic and copies ran while one was open for 22% of the time, Pallas kernels for 0%

commit v1 on v0

--- a/solution.py
+++ b/solution.py
@@ -1,3 +1,4 @@
+import functools
 import jax
 import jax.numpy as jnp
 from jax import lax
@@ -5,6 +6,43 @@
 
 LEAVES_DEV = 16
 NODES = 4
+
+
+def _match_things(page, out_dim, local_values):
+    finding = page.shape
+    all_rows = page.reshape(
+        *finding[:out_dim], local_values, finding[out_dim] // local_values, *finding[out_dim + 1 :]
+    )
+    s_next = jnp.moveaxis(all_rows, out_dim, 0)
+    return s_next
+
+
+def set_gates(tile_in, dim_no):
+    passed = list(tile_in.shape[1:])
+    passed[dim_no] *= tile_in.shape[0]
+    everything = jnp.moveaxis(tile_in, 0, dim_no).reshape(passed)
+    return everything
+
+
+def yards_keep_up(my_tile, lane_axis, t0, local_block):
+    vec_out = lax.axis_size(lane_axis)
+    seen_now = lax.axis_index(lane_axis)
+    frame_out, value_now = (vec_out, seen_now)
+    newest = _match_things(my_tile, t0, frame_out)
+    queue = [newest[value_now]]
+    for idx in range(1, frame_out):
+        carry_out = newest[value_now ^ idx]
+        side_arr = lax.ppermute(
+            carry_out, lane_axis, [(dev_i, dev_i ^ idx) for dev_i in range(frame_out)]
+        )
+        queue.append(side_arr)
+    raw_out = jnp.stack(queue, axis=0)
+    newest = raw_out[value_now ^ jnp.arange(frame_out)]
+    m_next = set_gates(newest, local_block)
+    return m_next
+
+
+proceed_numbers_over_axis = functools.partial(yards_keep_up, lane_axis="dom", t0=0, local_block=0)
 
 
 def cheb_points():
@@ -200,7 +238,7 @@
     described = jnp.concatenate([positions, leaf_row], axis=1)
     packed_blocks, packed_meta = pack_slots(block_owner, dom_count, capacity, (masked, described))
     owner_blocks, owner_meta = (
-        lax.all_to_all(packed_blocks, "dom", split_axis=0, concat_axis=0, tiled=True),
+        proceed_numbers_over_axis(packed_blocks),
         lax.all_to_all(packed_meta, "dom", split_axis=0, concat_axis=0, tiled=True),
     )
     arrived_blocks, arrived_meta = (

time: 454 us -> 457 us (level)
  blocking collectives: 85.7 us -> 9.38 us
  waiting for transfers between devices: 0.03 us -> 44.8 us
  starting transfers between devices: 17.3 us -> 46.7 us
  local copies, waits for them, and re-layouts: 53 us -> 58.1 us
    all_to_all x1 -> x0, blocking collectives: 76.3 us -> none  [boundary_part(): lax.all_to_all(packed_blocks, 'dom', split_axis=0, concat_axis=0, tiled=T...]
    ppermute x0 -> x7, waiting for transfers between devices: none -> 44.7 us  [yards_keep_up(): lax.ppermute(carry_out, lane_axis, [(dev_i, dev_i ^ idx) for dev_i in ran...]
    all_to_all x1, starting transfers between devices: 5.23 us -> 23.7 us  [interior_part(): lax.all_to_all(outgoing, ('dom', 'dir'), split_axis=0, concat_axis=0, til...]
    ppermute x0 -> x7, starting transfers between devices: none -> 10.9 us  [yards_keep_up(): lax.ppermute(carry_out, lane_axis, [(dev_i, dev_i ^ idx) for dev_i in ran...]
  transfers between devices with their start and end apart: 4 -> 11, of which waited for: 0 -> 6; matrix products, arithmetic and copies ran while one was open for 22% -> 22% of each run, Pallas kernels for 0% -> 0%
where the time goes in v1:
time: 457 us; the launch traced here: 450 us
  other arithmetic  106 us (23%)
  matrix products  96.8 us (21%)
  local copies, waits for them, and re-layouts  58.1 us (13%)
  loops' own time  56.8 us (12%)
  starting transfers between devices  46.7 us (10%)
  waiting for transfers between devices  44.8 us (10%)
  between operations  30.8 us (7%)
  blocking collectives  9.38 us (2%)
    another operation x1, loops' own time, expand_leaves(): sums, unused = lax.scan(one_group, (empty, empty), inputs)  56.8 us
    ppermute x7, waiting for transfers between devices, yards_keep_up(): lax.ppermute(carry_out, lane_axis, [(dev_i, dev_i ^ idx) for dev_i in ran...  44.7 us
    scatter-add x1, other arithmetic, interior_part(): jax.ops.segment_sum(stacked, connectivity.reshape(-1), num_segments=owned...  33.9 us
    div x10, other arithmetic, lagrange(): product * (points - node_values[other_node])  25.6 us
    dot_general x3, matrix products, one_group(): jnp.einsum('lg,gcqn->lcqn', selector, real_part, preferred_element_type=j...  24.6 us
    all_to_all x1, starting transfers between devices, interior_part(): lax.all_to_all(outgoing, ('dom', 'dir'), split_axis=0, concat_axis=0, til...  23.7 us
    dot_general x3, matrix products, one_group(): jnp.einsum('lg,gcqn->lcqn', selector, imag_part, preferred_element_type=j...  21.3 us
    dot_general x3, matrix products, one_group(): jnp.einsum('gcqb,gbn->gcqn', real_w, blocks_now, preferred_element_type=j...  20.9 us
  transfers between devices with their start and end apart: 11, of which 6 were waited for; matrix products, arithmetic and copies ran while one was open for 22% of the time, Pallas kernels for 0%

profile of v1, /device:TPU:1, one launch (start us, length us, event | category | flops | bytes accessed | tf_op | source)
XLA Modules:
  0.0 449.7 jit_solution(8631275246321632141)
XLA Ops:
  13.6 2.7 gather_fusion.3
  21.8 2.4 collective-permute-start.3
  25.2 4.1 collective-permute-done
  29.3 3.3 collective-permute-start.5
  32.7 13.5 %collective-permute-done.1 = bf16[12,128,128]{2,1,0:T(8,128)(2,1)S(1)} collective-permute-done((bf16[12,128,128]{2,1,0:T(8,128)(2,1)S(1)}, bf16[12,128,128]{2,1,0:T(8,128)(2,1)S(1)}, u32[]{:S(2)}, u32[]{:S(2)}) %collective-permute-start.1) | collective-permute-done | bytes 393248 | tf_op jit(solution)/shard_map/ppermute | solution.py:35
  46.9 7.1 %collective-permute-done.2 = bf16[12,128,128]{2,1,0:T(8,128)(2,1)S(1)} collective-permute-done((bf16[12,128,128]{2,1,0:T(8,128)(2,1)S(1)}, bf16[12,128,128]{2,1,0:T(8,128)(2,1)S(1)}, u32[]{:S(2)}, u32[]{:S(2)}) %collective-permute-start.2) | collective-permute-done | bytes 393248 | tf_op jit(solution)/shard_map/ppermute | solution.py:35
  54.7 11.3 %collective-permute-done.5 = bf16[12,128,128]{2,1,0:T(8,128)(2,1)S(1)} collective-permute-done((bf16[12,128,128]{2,1,0:T(8,128)(2,1)S(1)}, bf16[12,128,128]{2,1,0:T(8,128)(2,1)S(1)}, u32[]{:S(2)}, u32[]{:S(2)}) %collective-permute-start.5) | collective-permute-done | bytes 393248 | tf_op jit(solution)/shard_map/ppermute | solution.py:35
  66.0 8.3 %collective-permute-done.6 = bf16[12,128,128]{2,1,0:T(8,128)(2,1)S(1)} collective-permute-done((bf16[12,128,128]{2,1,0:T(8,128)(2,1)S(1)}, bf16[12,128,128]{2,1,0:T(8,128)(2,1)S(1)}, u32[]{:S(2)}, u32[]{:S(2)}) %collective-permute-start.6) | collective-permute-done | bytes 393248 | tf_op jit(solution)/shard_map/ppermute | solution.py:35
  74.4 2.6 gather_fusion.4
  78.1 4.3 gather_fusion
  82.4 23.7 %all-to-all-start = ((bf16[32,32,128]{2,1,0:T(8,128)(2,1)}), bf16[32,32,128]{2,1,0:T(8,128)(2,1)S(1)}, u32[]{:S(2)}, u32[]{:S(2)}) async-start(bf16[32,32,128]{2,1,0:T(8,128)(2,1)} %bitcast.2), calls=%async_computation | async-start | bytes 524288 | tf_op jit(solution)/shard_map/all_to_all | solution.py:144
  122.2 2.5 fusion.102
  133.2 3.3 copy.39
  137.3 5.7 %all-to-all-start.2 = ((bf16[96,4,128]{2,1,0:T(4,128)(2,1)}), bf16[96,4,128]{2,1,0:T(4,128)(2,1)S(1)}, u32[]{:S(2)}, u32[]{:S(2)}) async-start(bf16[96,4,128]{2,1,0:T(4,128)(2,1)} %gather_fusion.2), calls=%async_computation.2 | async-start | bytes 196608 | tf_op jit(solution)/shard_map/all_to_all | solution.py:242
  143.2 18.1 %gather_fusion.1 = bf16[6144,128]{1,0:T(8,128)(2,1)S(1)} fusion(bf16[3072,128]{1,0:T(8,128)(2,1)S(1)} %pad_maximum_fusion.3, s32[6144]{0:T(1024)S(1)} %broadcast_clamp_fusion), kind=kCustom, calls=%fused_computation.1 | custom fusion | bytes 3170304 | tf_op jit(solution)/shard_map/gather | solution.py:146
  170.9 33.9 %scatter_custom_fusion = f32[3072,128]{1,0:T(8,128)S(1)} fusion(s32[6144]{0:T(1024)} %reshape.1088, f32[6144,128]{1,0:T(8,128)} %bitcast.330, f32[]{:T(128)} %constant.163.clone.1), kind=kCustom, calls=%fused_computation.119 | custom fusion | flops 786432 | bytes 1573376 | tf_op jit(solution)/shard_map/scatter-add | solution.py:155
  205.7 6.4 %all-to-all-start.1 = ((f32[32,32,128]{2,1,0:T(8,128)}), f32[32,32,128]{2,1,0:T(8,128)S(1)}, u32[]{:S(2)}, u32[]{:S(2)}) async-start(f32[32,32,128]{2,1,0:T(8,128)} %bitcast.52), calls=%async_computation.1 | async-start | bytes 1048576 | tf_op jit(solution)/shard_map/all_to_all | solution.py:159
  213.5 9.4 %all_gather.6 = bf16[384,4,128]{2,1,0:T(4,128)(2,1)S(1)} all-gather(bf16[96,4,128]{2,1,0:T(4,128)(2,1)S(1)} %all-to-all-done.2), channel_id=1, replica_groups=mesh['dom'=8,'dir'=4] {'dir'}, dimensions={0}, use_global_device_ids=true | all-gather | bytes 491520 | tf_op jit(solution)/shard_map/all_gather | solution.py:246
  222.9 6.9 %fusion.84 = s32[384]{0:T(512)S(1)} fusion(bf16[384,4,128]{2,1,0:T(4,128)(2,1)S(1)} %all_gather.6), kind=kLoop, calls=%fused_computation.194 | loop fusion | flops 384 | bytes 2304 | tf_op jit(solution)/shard_map/convert_element_type | solution.py:179
  230.6 7.3 %scatter_custom_fusion.1 = f32[2049,128]{1,0:T(8,128)S(1)} fusion(s32[1024]{0:T(1024)} %reshape.1096, f32[1024,128]{1,0:T(8,128)} %bitcast.329, f32[]{:T(128)} %constant.163.clone.1), kind=kCustom, calls=%fused_computation.121 | custom fusion | flops 131072 | bytes 1049600 | tf_op jit(solution)/shard_map/scatter-add | solution.py:166
  237.9 2.3 slice_add_fusion
  240.2 183.6 %while.13 = (s32[]{:T(128)}, f32[16,4,64,128]{3,0,2,1:T(8,128)S(1)}, f32[16,4,64,128]{3,0,2,1:T(8,128)}, s32[3,128]{1,0:T(4,128)S(1)}, bf16[3,128,3,128]{3,1,2,0...) while((s32[]{:T(128)}, ...), condition=%wide.region_6.7_spmd.clone, body=%wide.region_5.6_spmd.clone.sunk | while | flops 2447904768 | bytes 113871504 | solution.py:210
  263.4 2.6 multiply_divide_fusion.15
  269.8 2.6 multiply_divide_fusion.16
  274.4 2.6 multiply_divide_fusion.17
  281.3 7.0 %fusion.152 = bf16[128,4,64,128]{3,2,1,0:T(8,128)(2,1)} fusion(f32[128,4,128]{2,1,0:T(4,128)S(1)} %get-tuple-element.274, f32[128,64,128]{2,1,0:T(8,128)S(1)} %bitcast.320, bf16[3,128,128,128]{3,2,1,0:T(8,128)(2,1)} %get-tuple-element.314, s32[]{:T(128)S(6)} %copy.85), kind=kOutput, calls=%fused_computation.21.clone.1 | convolution fusion | flops 1086324736 | bytes 17039364 | tf_op jit(solution)/shard_map/while/body/eval_jaxpr/gcqb,gbn->gcqn/dot_general | solution.py:189
  288.2 8.2 %select_add_fusion.4 = f32[16,4,64,128]{3,0,2,1:T(8,128)S(1)} fusion(f32[16,4,64,128]{3,0,2,1:T(8,128)S(1)} %get-tuple-element.300, bf16[128,4,64,128]{3,2,1,0:T(8,128)(2,1)} %fusion.152, pred[]{:T(512)S(6)} %compare.55, s32[128]{0:T(128)S(1)} %fusion.153), kind=kOutput, calls=%fused_computation.27.clone.1 | convolution fusion | flops 135268352 | bytes 12583425 | tf_op jit(solution)/shard_map/while/body/eval_jaxpr/lg,gcqn->lcqn/dot_general | solution.py:196
  296.9 4.8 %fusion.154 = bf16[128,4,64,128]{3,2,1,0:T(8,128)(2,1)S(1)} fusion(f32[128,4,128]{2,1,0:T(4,128)S(1)} %get-tuple-element.289, f32[128,64,128]{2,1,0:T(8,128)S(1)} %neg.19, bf16[3,128,128,128]{3,2,1,0:T(8,128)(2,1)} %get-tuple-element.314, s32[]{:T(128)S(6)} %copy.85), kind=kOutput, calls=%fused_computation.20.clone.1 | convolution fusion | flops 1086324736 | bytes 17039364 | tf_op jit(solution)/shard_map/while/body/eval_jaxpr/gcqb,gbn->gcqn/dot_general | solution.py:192
  301.7 6.0 %select_add_fusion.5 = f32[16,4,64,128]{3,0,2,1:T(8,128)} fusion(f32[16,4,64,128]{3,0,2,1:T(8,128)} %get-tuple-element.301, bf16[128,4,64,128]{3,2,1,0:T(8,128)(2,1)S(1)} %fusion.154, pred[]{:T(512)S(6)} %compare.55, s32[128]{0:T(128)S(1)} %fusion.153), kind=kOutput, calls=%fused_computation.26.clone.1 | convolution fusion | flops 135268352 | bytes 12583425 | tf_op jit(solution)/shard_map/while/body/eval_jaxpr/lg,gcqn->lcqn/dot_general | solution.py:199
  319.7 2.6 multiply_divide_fusion.15
  326.1 2.6 multiply_divide_fusion.16
  330.8 2.6 multiply_divide_fusion.17
  337.6 7.0 %fusion.152 = bf16[128,4,64,128]{3,2,1,0:T(8,128)(2,1)} fusion(f32[128,4,128]{2,1,0:T(4,128)S(1)} %get-tuple-element.274, f32[128,64,128]{2,1,0:T(8,128)S(1)} %bitcast.320, bf16[3,128,128,128]{3,2,1,0:T(8,128)(2,1)} %get-tuple-element.314, s32[]{:T(128)S(6)} %copy.85), kind=kOutput, calls=%fused_computation.21.clone.1 | convolution fusion | flops 1086324736 | bytes 17039364 | tf_op jit(solution)/shard_map/while/body/eval_jaxpr/gcqb,gbn->gcqn/dot_general | solution.py:189
  344.6 8.2 %select_add_fusion.4 = f32[16,4,64,128]{3,0,2,1:T(8,128)S(1)} fusion(f32[16,4,64,128]{3,0,2,1:T(8,128)S(1)} %get-tuple-element.300, bf16[128,4,64,128]{3,2,1,0:T(8,128)(2,1)} %fusion.152, pred[]{:T(512)S(6)} %compare.55, s32[128]{0:T(128)S(1)} %fusion.153), kind=kOutput, calls=%fused_computation.27.clone.1 | convolution fusion | flops 135268352 | bytes 12583425 | tf_op jit(solution)/shard_map/while/body/eval_jaxpr/lg,gcqn->lcqn/dot_general | solution.py:196
  353.2 4.8 %fusion.154 = bf16[128,4,64,128]{3,2,1,0:T(8,128)(2,1)S(1)} fusion(f32[128,4,128]{2,1,0:T(4,128)S(1)} %get-tuple-element.289, f32[128,64,128]{2,1,0:T(8,128)S(1)} %neg.19, bf16[3,128,128,128]{3,2,1,0:T(8,128)(2,1)} %get-tuple-element.314, s32[]{:T(128)S(6)} %copy.85), kind=kOutput, calls=%fused_computation.20.clone.1 | convolution fusion | flops 1086324736 | bytes 17039364 | tf_op jit(solution)/shard_map/while/body/eval_jaxpr/gcqb,gbn->gcqn/dot_general | solution.py:192
  358.1 7.6 %select_add_fusion.5 = f32[16,4,64,128]{3,0,2,1:T(8,128)} fusion(f32[16,4,64,128]{3,0,2,1:T(8,128)} %get-tuple-element.301, bf16[128,4,64,128]{3,2,1,0:T(8,128)(2,1)S(1)} %fusion.154, pred[]{:T(512)S(6)} %compare.55, s32[128]{0:T(128)S(1)} %fusion.153), kind=kOutput, calls=%fused_computation.26.clone.1 | convolution fusion | flops 135268352 | bytes 12583425 | tf_op jit(solution)/shard_map/while/body/eval_jaxpr/lg,gcqn->lcqn/dot_general | solution.py:199
  377.6 2.6 multiply_divide_fusion.15
  384.0 2.6 multiply_divide_fusion.16
  388.7 2.6 multiply_divide_fusion.17
  395.5 7.0 %fusion.152 = bf16[128,4,64,128]{3,2,1,0:T(8,128)(2,1)} fusion(f32[128,4,128]{2,1,0:T(4,128)S(1)} %get-tuple-element.274, f32[128,64,128]{2,1,0:T(8,128)S(1)} %bitcast.320, bf16[3,128,128,128]{3,2,1,0:T(8,128)(2,1)} %get-tuple-element.314, s32[]{:T(128)S(6)} %copy.85), kind=kOutput, calls=%fused_computation.21.clone.1 | convolution fusion | flops 1086324736 | bytes 17039364 | tf_op jit(solution)/shard_map/while/body/eval_jaxpr/gcqb,gbn->gcqn/dot_general | solution.py:189
  402.5 8.2 %select_add_fusion.4 = f32[16,4,64,128]{3,0,2,1:T(8,128)S(1)} fusion(f32[16,4,64,128]{3,0,2,1:T(8,128)S(1)} %get-tuple-element.300, bf16[128,4,64,128]{3,2,1,0:T(8,128)(2,1)} %fusion.152, pred[]{:T(512)S(6)} %compare.55, s32[128]{0:T(128)S(1)} %fusion.153), kind=kOutput, calls=%fused_computation.27.clone.1 | convolution fusion | flops 135268352 | bytes 12583425 | tf_op jit(solution)/shard_map/while/body/eval_jaxpr/lg,gcqn->lcqn/dot_general | solution.py:196
  411.2 4.8 %fusion.154 = bf16[128,4,64,128]{3,2,1,0:T(8,128)(2,1)S(1)} fusion(f32[128,4,128]{2,1,0:T(4,128)S(1)} %get-tuple-element.289, f32[128,64,128]{2,1,0:T(8,128)S(1)} %neg.19, bf16[3,128,128,128]{3,2,1,0:T(8,128)(2,1)} %get-tuple-element.314, s32[]{:T(128)S(6)} %copy.85), kind=kOutput, calls=%fused_computation.20.clone.1 | convolution fusion | flops 1086324736 | bytes 17039364 | tf_op jit(solution)/shard_map/while/body/eval_jaxpr/gcqb,gbn->gcqn/dot_general | solution.py:192
  416.0 7.6 %select_add_fusion.5 = f32[16,4,64,128]{3,0,2,1:T(8,128)} fusion(f32[16,4,64,128]{3,0,2,1:T(8,128)} %get-tuple-element.301, bf16[128,4,64,128]{3,2,1,0:T(8,128)(2,1)S(1)} %fusion.154, pred[]{:T(512)S(6)} %compare.55, s32[128]{0:T(128)S(1)} %fusion.153), kind=kOutput, calls=%fused_computation.26.clone.1 | convolution fusion | flops 135268352 | bytes 12583425 | tf_op jit(solution)/shard_map/while/body/eval_jaxpr/lg,gcqn->lcqn/dot_general | solution.py:199
  423.8 2.1 fusion.35
  426.0 3.8 convolution_bitcast_fusion
  429.8 3.8 convolution_bitcast_fusion.2
  433.7 3.8 fusion.33
  437.5 4.1 fusion.31
  (250 shorter events, 61.3 us)
Async XLA Ops:
  7.2 233.1 %all-gather.2.cloned.1.call-start = ((), (), s32[]{:S(2)}) async-start(), calls=%async_computation.3 | async-start | bytes 15728640 | tf_op jit(solution)/shard_map/all_gather | solution.py:245
  18.4 10.9 %collective-permute-start = (bf16[12,128,128]{2,1,0:T(8,128)(2,1)S(1)}, bf16[12,128,128]{2,1,0:T(8,128)(2,1)S(1)}, u32[]{:S(2)}, u32[]{:S(2)}) collective-permute-start(bf16[12,128,128]{2,1,0:T(8,128)(2,1)S(1)} %get-tuple-element.127), channel_id=1, source_target_pairs={{0,4},{4,0},{8,12},{12,8},{16,20},{20,16},{24,28},{28,24},{1,5},{5... | collective-permute-start | bytes 1179656 | tf_op jit(solution)/shard_map/ppermute | solution.py:35
  20.5 25.6 %collective-permute-start.1 = (bf16[12,128,128]{2,1,0:T(8,128)(2,1)S(1)}, bf16[12,128,128]{2,1,0:T(8,128)(2,1)S(1)}, u32[]{:S(2)}, u32[]{:S(2)}) collective-permute-start(bf16[12,128,128]{2,1,0:T(8,128)(2,1)S(1)} %get-tuple-element.126), channel_id=1, source_target_pairs={{0,8},{4,12},{8,0},{12,4},{16,24},{20,28},{24,16},{28,20},{1,9},{5... | collective-permute-start | bytes 1179656 | tf_op jit(solution)/shard_map/ppermute | solution.py:35
  21.8 32.2 %collective-permute-start.2 = (bf16[12,128,128]{2,1,0:T(8,128)(2,1)S(1)}, bf16[12,128,128]{2,1,0:T(8,128)(2,1)S(1)}, u32[]{:S(2)}, u32[]{:S(2)}) collective-permute-start(bf16[12,128,128]{2,1,0:T(8,128)(2,1)S(1)} %get-tuple-element.125), channel_id=1, source_target_pairs={{0,12},{4,8},{8,4},{12,0},{16,28},{20,24},{24,20},{28,16},{1,13},{... | collective-permute-start | bytes 1179656 | tf_op jit(solution)/shard_map/ppermute | solution.py:35
  21.8 32.3 %collective-permute-start.3 = (bf16[12,128,128]{2,1,0:T(8,128)(2,1)S(1)}, bf16[12,128,128]{2,1,0:T(8,128)(2,1)S(1)}, u32[]{:S(2)}, u32[]{:S(2)}) collective-permute-start(bf16[12,128,128]{2,1,0:T(8,128)(2,1)S(1)} %get-tuple-element.124), channel_id=1, source_target_pairs={{0,16},{4,20},{8,24},{12,28},{16,0},{20,4},{24,8},{28,12},{1,17},{... | collective-permute-start | bytes 1179656 | tf_op jit(solution)/shard_map/ppermute | solution.py:35
  24.2 30.4 %collective-permute-start.4 = (bf16[12,128,128]{2,1,0:T(8,128)(2,1)S(1)}, bf16[12,128,128]{2,1,0:T(8,128)(2,1)S(1)}, u32[]{:S(2)}, u32[]{:S(2)}) collective-permute-start(bf16[12,128,128]{2,1,0:T(8,128)(2,1)S(1)} %get-tuple-element.123), channel_id=1, source_target_pairs={{0,20},{4,16},{8,28},{12,24},{16,4},{20,0},{24,12},{28,8},{1,21},{... | collective-permute-start | bytes 1179656 | tf_op jit(solution)/shard_map/ppermute | solution.py:35
  29.3 36.7 %collective-permute-start.5 = (bf16[12,128,128]{2,1,0:T(8,128)(2,1)S(1)}, bf16[12,128,128]{2,1,0:T(8,128)(2,1)S(1)}, u32[]{:S(2)}, u32[]{:S(2)}) collective-permute-start(bf16[12,128,128]{2,1,0:T(8,128)(2,1)S(1)} %get-tuple-element.122), channel_id=1, source_target_pairs={{0,24},{4,28},{8,16},{12,20},{16,8},{20,12},{24,0},{28,4},{1,25},{... | collective-permute-start | bytes 1179656 | tf_op jit(solution)/shard_map/ppermute | solution.py:35
  46.1 28.2 %collective-permute-start.6 = (bf16[12,128,128]{2,1,0:T(8,128)(2,1)S(1)}, bf16[12,128,128]{2,1,0:T(8,128)(2,1)S(1)}, u32[]{:S(2)}, u32[]{:S(2)}) collective-permute-start(bf16[12,128,128]{2,1,0:T(8,128)(2,1)S(1)} %get-tuple-element.121), channel_id=1, source_target_pairs={{0,28},{4,24},{8,20},{12,16},{16,12},{20,8},{24,4},{28,0},{1,29},{... | collective-permute-start | bytes 1179656 | tf_op jit(solution)/shard_map/ppermute | solution.py:35
  77.0 44.9 %copy-start.12 = (s32[6,1024]{1,0:T(8,128)S(1)}, s32[6,1024]{1,0:T(8,128)}, u32[]{:S(2)}) copy-start(s32[6,1024]{1,0:T(8,128)} %param.15) | copy-start | bytes 73732
  77.0 44.9 %copy-start.57 = (s32[32]{0:T(128)S(1)}, s32[32]{0:T(128)}, u32[]{:S(2)}) copy-start(s32[32]{0:T(128)} %param.22) | copy-start | bytes 388
  77.0 44.9 %copy-start.16 = (bf16[32,3,128]{2,0,1:T(8,128)(2,1)S(1)}, bf16[32,3,128]{2,0,1:T(8,128)(2,1)}, u32[]{:S(2)}) copy-start(bf16[32,3,128]{2,0,1:T(8,128)(2,1)} %param.19) | copy-start | bytes 73732
  77.0 48.4 %copy-start.15 = (f32[3,4]{1,0:T(4,128)S(1)}, f32[3,4]{1,0:T(4,128)}, u32[]{:S(2)}) copy-start(f32[3,4]{1,0:T(4,128)} %param.23) | copy-start | bytes 148
  77.0 49.0 %copy-start.11 = (f32[36,1024]{1,0:T(8,128)S(1)}, f32[36,1024]{1,0:T(8,128)}, u32[]{:S(2)}) copy-start(f32[36,1024]{1,0:T(8,128)} %param.16) | copy-start | bytes 442372
  78.1 49.2 %copy-start.14 = (s32[32,32]{1,0:T(8,128)S(1)}, s32[32,32]{1,0:T(8,128)}, u32[]{:S(2)}) copy-start(s32[32,32]{1,0:T(8,128)} %param.14) | copy-start | bytes 12292
  82.4 54.9 %all-to-all-start = ((bf16[32,32,128]{2,1,0:T(8,128)(2,1)}), bf16[32,32,128]{2,1,0:T(8,128)(2,1)S(1)}, u32[]{:S(2)}, u32[]{:S(2)}) async-start(bf16[32,32,128]{2,1,0:T(8,128)(2,1)} %bitcast.2), calls=%async_computation | async-start | bytes 524288 | tf_op jit(solution)/shard_map/all_to_all | solution.py:144
  122.2 7.9 %copy-start.49 = (f32[3,64]{1,0:T(4,128)}, f32[3,64]{1,0:T(4,128)S(1)}, u32[]{:S(2)}) copy-start(f32[3,64]{1,0:T(4,128)S(1)} %get-tuple-element.184) | copy-start | bytes 2308
  137.3 68.4 %all-to-all-start.2 = ((bf16[96,4,128]{2,1,0:T(4,128)(2,1)}), bf16[96,4,128]{2,1,0:T(4,128)(2,1)S(1)}, u32[]{:S(2)}, u32[]{:S(2)}) async-start(bf16[96,4,128]{2,1,0:T(4,128)(2,1)} %gather_fusion.2), calls=%async_computation.2 | async-start | bytes 196608 | tf_op jit(solution)/shard_map/all_to_all | solution.py:242
  143.1 18.3 %copy-start.24 = (f32[1,1024]{1,0:T(1,128)S(1)}, f32[1,1024]{1,0:T(1,128)}, u32[]{:S(2)}) copy-start(f32[1,1024]{1,0:T(1,128)} %get-tuple-element.161) | copy-start | bytes 12292
  143.1 18.3 %copy-start.25 = (f32[1,1024]{1,0:T(1,128)S(1)}, f32[1,1024]{1,0:T(1,128)}, u32[]{:S(2)}) copy-start(f32[1,1024]{1,0:T(1,128)} %get-tuple-element.162) | copy-start | bytes 12292
  143.1 18.3 %copy-start.26 = (f32[1,1024]{1,0:T(1,128)S(1)}, f32[1,1024]{1,0:T(1,128)}, u32[]{:S(2)}) copy-start(f32[1,1024]{1,0:T(1,128)} %get-tuple-element.163) | copy-start | bytes 12292
  143.1 18.3 %copy-start.27 = (f32[1,1024]{1,0:T(1,128)S(1)}, f32[1,1024]{1,0:T(1,128)}, u32[]{:S(2)}) copy-start(f32[1,1024]{1,0:T(1,128)} %get-tuple-element.164) | copy-start | bytes 12292
  143.1 18.3 %copy-start.28 = (f32[1,1024]{1,0:T(1,128)S(1)}, f32[1,1024]{1,0:T(1,128)}, u32[]{:S(2)}) copy-start(f32[1,1024]{1,0:T(1,128)} %get-tuple-element.165) | copy-start | bytes 12292
  143.1 18.3 %copy-start.29 = (f32[1,1024]{1,0:T(1,128)S(1)}, f32[1,1024]{1,0:T(1,128)}, u32[]{:S(2)}) copy-start(f32[1,1024]{1,0:T(1,128)} %get-tuple-element.166) | copy-start | bytes 12292
  143.1 19.5 %copy-start.18 = (f32[1,1024]{1,0:T(1,128)S(1)}, f32[1,1024]{1,0:T(1,128)}, u32[]{:S(2)}) copy-start(f32[1,1024]{1,0:T(1,128)} %get-tuple-element.155) | copy-start | bytes 12292
  143.2 19.5 %copy-start.19 = (f32[1,1024]{1,0:T(1,128)S(1)}, f32[1,1024]{1,0:T(1,128)}, u32[]{:S(2)}) copy-start(f32[1,1024]{1,0:T(1,128)} %get-tuple-element.156) | copy-start | bytes 12292
  143.2 19.5 %copy-start.20 = (f32[1,1024]{1,0:T(1,128)S(1)}, f32[1,1024]{1,0:T(1,128)}, u32[]{:S(2)}) copy-start(f32[1,1024]{1,0:T(1,128)} %get-tuple-element.157) | copy-start | bytes 12292
  143.2 19.5 %copy-start.21 = (f32[1,1024]{1,0:T(1,128)S(1)}, f32[1,1024]{1,0:T(1,128)}, u32[]{:S(2)}) copy-start(f32[1,1024]{1,0:T(1,128)} %get-tuple-element.158) | copy-start | bytes 12292
  143.2 19.5 %copy-start.22 = (f32[1,1024]{1,0:T(1,128)S(1)}, f32[1,1024]{1,0:T(1,128)}, u32[]{:S(2)}) copy-start(f32[1,1024]{1,0:T(1,128)} %get-tuple-element.159) | copy-start | bytes 12292
  143.2 19.5 %copy-start.23 = (f32[1,1024]{1,0:T(1,128)S(1)}, f32[1,1024]{1,0:T(1,128)}, u32[]{:S(2)}) copy-start(f32[1,1024]{1,0:T(1,128)} %get-tuple-element.160) | copy-start | bytes 12292
  161.4 3.9 copy-start.40
  161.4 3.9 copy-start.41
  161.4 3.9 copy-start.42
  161.4 3.9 copy-start.43
  161.4 3.9 copy-start.44
  167.9 44.2 %copy-start.51 = (f32[4]{0:T(128)S(1)}, f32[4]{0:T(128)}, u32[]{:S(2)}) copy-start(f32[4]{0:T(128)} %get-tuple-element.177) | copy-start | bytes 52
  167.9 44.2 %copy-start.52 = (f32[4]{0:T(128)S(1)}, f32[4]{0:T(128)}, u32[]{:S(2)}) copy-start(f32[4]{0:T(128)} %get-tuple-element.178) | copy-start | bytes 52
  167.9 44.2 %copy-start.53 = (f32[4]{0:T(128)S(1)}, f32[4]{0:T(128)}, u32[]{:S(2)}) copy-start(f32[4]{0:T(128)} %get-tuple-element.179) | copy-start | bytes 52
  167.9 44.2 %copy-start.54 = (f32[64]{0:T(128)S(1)}, f32[64]{0:T(128)}, u32[]{:S(2)}) copy-start(f32[64]{0:T(128)} %get-tuple-element.180) | copy-start | bytes 772
  167.9 44.2 %copy-start.55 = (f32[64]{0:T(128)S(1)}, f32[64]{0:T(128)}, u32[]{:S(2)}) copy-start(f32[64]{0:T(128)} %get-tuple-element.181) | copy-start | bytes 772
  167.9 44.2 %copy-start.56 = (f32[64]{0:T(128)S(1)}, f32[64]{0:T(128)}, u32[]{:S(2)}) copy-start(f32[64]{0:T(128)} %get-tuple-element.182) | copy-start | bytes 772
  168.0 44.3 %copy-start.50 = (f32[3,64]{1,0:T(4,128)S(1)}, f32[3,64]{1,0:T(4,128)}, u32[]{:S(2)}) copy-start(f32[3,64]{1,0:T(4,128)} %copy-done.49) | copy-start | bytes 2308
  204.8 7.8 %copy-start.3 = (f32[3072,128]{1,0:T(8,128)}, f32[3072,128]{1,0:T(8,128)S(1)}, u32[]{:S(2)}) copy-start(f32[3072,128]{1,0:T(8,128)S(1)} %scatter_custom_fusion) | copy-start | bytes 4718596
  205.7 24.1 %all-to-all-start.1 = ((f32[32,32,128]{2,1,0:T(8,128)}), f32[32,32,128]{2,1,0:T(8,128)S(1)}, u32[]{:S(2)}, u32[]{:S(2)}) async-start(f32[32,32,128]{2,1,0:T(8,128)} %bitcast.52), calls=%async_computation.1 | async-start | bytes 1048576 | tf_op jit(solution)/shard_map/all_to_all | solution.py:159
  213.5 26.7 %copy-start.2 = (f32[16,4,64,128]{3,0,2,1:T(8,128)S(1)}, f32[16,4,64,128]{3,0,2,1:T(8,128)}, u32[]{:S(2)}) copy-start(f32[16,4,64,128]{3,0,2,1:T(8,128)} %custom-call) | copy-start | bytes 6291460
  288.2 8.2 %copy-start.1 = (f32[128,4,4,4,128]{4,3,2,1,0:T(4,128)S(1)}, f32[128,4,4,4,128]{4,3,2,1,0:T(4,128)}, u32[]{:S(2)}) copy-start(f32[128,4,4,4,128]{4,3,2,1,0:T(4,128)} %copy-done) | copy-start | bytes 12582916 | tf_op jit(solution)/shard_map/while
  344.6 8.2 %copy-start.1 = (f32[128,4,4,4,128]{4,3,2,1,0:T(4,128)S(1)}, f32[128,4,4,4,128]{4,3,2,1,0:T(4,128)}, u32[]{:S(2)}) copy-start(f32[128,4,4,4,128]{4,3,2,1,0:T(4,128)} %copy-done) | copy-start | bytes 12582916 | tf_op jit(solution)/shard_map/while
  402.5 8.2 %copy-start.1 = (f32[128,4,4,4,128]{4,3,2,1,0:T(4,128)S(1)}, f32[128,4,4,4,128]{4,3,2,1,0:T(4,128)}, u32[]{:S(2)}) copy-start(f32[128,4,4,4,128]{4,3,2,1,0:T(4,128)} %copy-done) | copy-start | bytes 12582916 | tf_op jit(solution)/shard_map/while
  426.0 7.7 %copy-start.6 = (f32[8,64,64]{1,0,2:T(8,128)S(1)}, f32[8,64,64]{1,0,2:T(8,128)}, u32[]{:S(2)}) copy-start(f32[8,64,64]{1,0,2:T(8,128)} %copy.37) | copy-start | bytes 393220
  (25 other events, 71.8 us)
Sparse Core Ops, SparseCore 0:
  77.2 103.9 all-gather.1
